TPU v7x, 32 devices: a whole 2x2x4 slice. The times are simulated.
32 devices in a mesh: pipe: 4 (over y, x), dp: 8 (over z, core).
Axes of the slice: x: 2, y: 2, z: 4, core: 2. Of those that a mesh axis runs over, the one named last changes fastest.
Arguments:
- acts: bfloat16 [4, 2048, 3072], P('pipe', 'dp'), may hold values from -24 to 24, as said below
- grad: float32 [12288, 4096], P('pipe', 'dp'), may hold values from -6 to 6
- owner_of: int32 [4, 12], replicated, may hold values from 0 to 3, as said below
Outputs:
- precond: float32 [12288, 4096], P('pipe', 'dp')
- held_inverse: float32 [4, 24, 256, 256], P('pipe', None, 'dp')
Inputs may be any that keep to these rules, and one draw needn't show every extreme that they name: `acts`: column and token scales of the activations vary; entries lie within the range. `owner_of`: no section index owns more than 24 blocks in all, and some section index owns exactly 24.
All inputs are finite; a program needn't handle non-finite values.
Results may differ from a plain program's by a relative error of at most 0.0003.
Values sent between devices are 32-bit elements; how exact they have to be, the bound alone decides.
A program may use at most 128 MiB of HBM per device.

v0:
```python
import functools

import jax
import jax.numpy as jnp
from jax import lax
from jax.experimental import pallas as pl
from jax.experimental.pallas import tpu as pltpu
from jax.sharding import PartitionSpec as P

BLK = 256
HALF = BLK // 2
PACK = HALF + 8
HOST = 24
UNROLL = 1
MESH = pl.DeviceIdType.MESH

damping_ratio = 0.1
F32 = jnp.float32
BF16 = jnp.bfloat16
HIGHEST = lax.Precision.HIGHEST


def square_iota():
    rows = lax.broadcasted_iota(jnp.int32, (HALF, HALF), 0)
    cols = lax.broadcasted_iota(jnp.int32, (HALF, HALF), 1)
    return rows, cols


def pack_into(ref, m11, m21, m22):
    rows, cols = square_iota()
    diag = jnp.sum(jnp.where(rows == cols, m22, 0.0), axis=0, keepdims=True)
    ref[0:HALF, 0:HALF] = m21
    ref[0:HALF, HALF:BLK] = jnp.where(rows >= cols, m11, m22)
    ref[HALF:PACK, 0:HALF] = jnp.broadcast_to(diag, (PACK - HALF, HALF))
    ref[HALF:PACK, HALF:BLK] = jnp.zeros((PACK - HALF, HALF), F32)


def unpack(value):
    rows, cols = square_iota()
    m21 = value[0:HALF, 0:HALF]
    mixed = value[0:HALF, HALF:BLK]
    diag = value[HALF : HALF + 1, 0:HALF]
    turned = mixed.T
    m11 = jnp.where(rows >= cols, mixed, turned)
    m22 = jnp.where(rows < cols, mixed, jnp.where(rows == cols, diag, turned))
    return m11, m21, m22


def owner_plan(chips, nhalf):
    order = []
    for i in range((chips + 1) // 2):
        order.extend([i] if i == chips - 1 - i else [i, chips - 1 - i])
    return [order[t % chips] for t in range(nhalf)], [order.index(i) for i in range(chips)]


def look_up(table, index):
    return sum((index == i).astype(jnp.int32) * value for i, value in enumerate(table))


def greet(signals):
    barrier = pltpu.get_barrier_semaphore()
    for condition, device in signals:
        if condition is None:
            pl.semaphore_signal(barrier, inc=1, device_id=device, device_id_type=MESH)
        else:
            @pl.when(condition)
            def _():
                pl.semaphore_signal(barrier, inc=1, device_id=device, device_id_type=MESH)
    peers = sum(1 if condition is None else condition.astype(jnp.int32) for condition, _ in signals)
    pl.semaphore_wait(barrier, peers)


def reduce_kernel(n, nhalf, nown, acts, out, theirs, mine, from_pair, from_low, from_high,
                  pair_s, pair_r, line_s, low_r, high_r):
    chips = n // 2
    me = lax.axis_index("dp")
    core = lax.rem(me, 2)
    chip = me // 2
    pair = me + 1 - 2 * core
    low = (jnp.maximum(chip - 1, 0)) * 2 + core
    high = (jnp.minimum(chip + 1, chips - 1)) * 2 + core
    owners, places = owner_plan(chips, nhalf)

    greet([(None, {"dp": pair}), (chip > 0, {"dp": low}), (chip < chips - 1, {"dp": high})])

    def partial(block, ref):
        start = pl.multiple_of(block * BLK, BLK)
        x = acts[:, pl.ds(start, BLK)]
        full = lax.dot_general(x, x, (((0,), (0,)), ((), ())), preferred_element_type=F32)
        pack_into(ref, full[0:HALF, 0:HALF], full[HALF:BLK, 0:HALF], full[HALF:BLK, HALF:BLK])

    def pair_copy(t):
        return pltpu.make_async_remote_copy(
            src_ref=theirs.at[t], dst_ref=from_pair.at[t], send_sem=pair_s.at[t], recv_sem=pair_r.at[t],
            device_id={"dp": pair}, device_id_type=MESH,
        )

    def fold_pair(t):
        pair_copy(t).wait()
        mine[t] = mine[t] + from_pair[t]

    def upward(t):
        return pltpu.make_async_remote_copy(
            src_ref=mine.at[t], dst_ref=from_low.at[t], send_sem=line_s.at[t], recv_sem=low_r.at[t],
            device_id={"dp": high}, device_id_type=MESH,
        )

    def downward(t):
        return pltpu.make_async_remote_copy(
            src_ref=mine.at[t], dst_ref=from_high.at[t], send_sem=line_s.at[t], recv_sem=high_r.at[t],
            device_id={"dp": low}, device_id_type=MESH,
        )

    up = sorted((t for t in range(nhalf) if owners[t] > 0), key=lambda t: -owners[t])
    down = sorted((t for t in range(nhalf) if owners[t] < chips - 1), key=lambda t: owners[t])

    turns = sorted(range(nhalf), key=lambda t: (min(up.index(t) if t in up else nhalf, down.index(t) if t in down else nhalf), t))

    @pl.loop(0, nhalf + chips)
    def _(tick):
        for turn in (2 * tick, 2 * tick + 1):
            @pl.when(turn < nhalf)
            def _():
                t = look_up(turns, turn)
                partial(2 * t + 1 - core, theirs.at[t])
                pair_copy(t).start()
                partial(2 * t + core, mine.at[t])

        i = tick - 1 - chip
        t = look_up(up, i)

        @pl.when((i >= 0) & (i < len(up)) & (look_up(owners, t) > chip))
        def _():
            fold_pair(t)

            @pl.when(chip > 0)
            def _():
                upward(t).wait_recv()
                mine[t] = mine[t] + from_low[t]

            upward(t).start()

        j = tick - 1 - (chips - 1 - chip)
        u = look_up(down, j)

        @pl.when((j >= 0) & (j < len(down)) & (look_up(owners, u) < chip))
        def _():
            fold_pair(u)

            @pl.when(chip < chips - 1)
            def _():
                downward(u).wait_recv()
                mine[u] = mine[u] + from_high[u]

            downward(u).start()

    place = look_up(places, chip)
    for slot in range(nown):
        t = slot * chips + place

        @pl.when(t < nhalf)
        def _():
            fold_pair(t)
            out[slot] = mine[t]

            @pl.when(chip > 0)
            def _():
                upward(t).wait_recv()
                out[slot] = out[slot] + from_low[t]

            @pl.when(chip < chips - 1)
            def _():
                downward(t).wait_recv()
                out[slot] = out[slot] + from_high[t]

        @pl.when(t >= nhalf)
        def _():
            rows, cols = square_iota()
            eye = jnp.where(rows == cols, 1.0, 0.0)
            pack_into(out.at[slot], eye, jnp.zeros((HALF, HALF), F32), eye)

    for t in range(nhalf):
        @pl.when(chip != owners[t])
        def _():
            upward(t).wait_send()


def dot3(a, b, contract):
    return jnp.stack([
        lax.dot_general(a[i], b[i], (contract, ((), ())), precision=HIGHEST, preferred_element_type=F32)
        for i in range(a.shape[0])
    ])


def sweep_inverse(a):
    count = a.shape[0]
    panel_shape = (count, 8, HALF)
    sub = lax.broadcasted_iota(jnp.int32, panel_shape, 1)
    lane = lax.broadcasted_iota(jnp.int32, panel_shape, 2)
    all_lanes = lax.broadcasted_iota(jnp.int32, (count, HALF, HALF), 2)

    def columns_of(top, first):
        return tuple(jnp.broadcast_to(top[:, :, k : k + 1], panel_shape) for k in range(first, first + 8))

    def panel(_, state):
        a, cols = state
        cols = list(cols)
        top = a[:, 0:8, :]
        for k in range(8):
            here = cols[k]
            inv = jnp.broadcast_to(1.0 / here[:, k : k + 1, :], panel_shape)
            row = jnp.broadcast_to(top[:, k : k + 1, :], panel_shape) * inv
            at_row = sub == k
            new = jnp.where(at_row, row, top - here * row)
            edge = jnp.where(at_row, inv, -here * inv)
            top = jnp.where(lane == k, edge, new)
            for j in range(k + 1, 8):
                across = jnp.broadcast_to(cols[j][:, k : k + 1, :], panel_shape) * inv
                cols[j] = jnp.where(at_row, across, cols[j] - here * across)
        top = jnp.where(lane < 8, -top, top)
        rest = a - jnp.stack([
            lax.dot_general(a[i, 0:8, :], top[i], (((0,), (0,)), ((), ())), precision=HIGHEST, preferred_element_type=F32)
            for i in range(count)
        ])
        ahead = columns_of(rest[:, 8:16, :], 8)
        tall = jnp.concatenate([top, jnp.zeros((count, HALF - 8, HALF), F32)], axis=1)
        turned = jnp.stack([tall[i].T for i in range(count)])
        rest = jnp.where(all_lanes < 8, turned, rest)
        a = jnp.concatenate([rest[:, 8:, :], top], axis=1)
        return pltpu.roll(a, HALF - 8, 2), ahead

    return -lax.fori_loop(0, HALF // 8, panel, (a, columns_of(a[:, 0:8, :], 0)), unroll=UNROLL)[0]


def invert_kernel(tokens, packed, out):
    count = packed.shape[0]
    rows, cols = square_iota()
    parts = [unpack(packed[i] / tokens) for i in range(count)]
    m11 = jnp.stack([p[0] for p in parts])
    m21 = jnp.stack([p[1] for p in parts])
    m22 = jnp.stack([p[2] for p in parts])
    eye = rows == cols
    trace = jnp.sum(jnp.where(eye, m11 + m22, 0.0), axis=(1, 2), keepdims=True)
    damping = jnp.where(eye, damping_ratio * trace / BLK, 0.0)
    x11 = sweep_inverse(m11 + damping)
    g = dot3(m21, x11, ((1,), (0,)))
    schur = m22 + damping - dot3(g, m21, ((1,), (1,)))
    y = sweep_inverse(schur)
    b21 = -dot3(y, g, ((1,), (0,)))
    b11 = x11 - dot3(g, b21, ((0,), (0,)))
    for i in range(count):
        pack_into(out.at[i], b11[i], b21[i], y[i])


def spread_kernel(n, sections, nhalf, nown, packed, full, rows_out, landed, low_s, high_s, near_r, pair_s, side_s, side_r):
    chips = n // 2
    share = BLK // n
    me = lax.axis_index("dp")
    section = lax.axis_index("pipe")
    core = lax.rem(me, 2)
    chip = me // 2
    pair = me + 1 - 2 * core
    low = (jnp.maximum(chip - 1, 0)) * 2 + core
    high = (jnp.minimum(chip + 1, chips - 1)) * 2 + core
    owners, places = owner_plan(chips, nhalf)

    greet(
        [(None, {"dp": pair}), (chip > 0, {"dp": low}), (chip < chips - 1, {"dp": high})]
        + [(None, {"pipe": lax.rem(section + step, sections)}) for step in range(1, sections)]
    )

    def send(source, t, half, target, sem):
        block = 2 * t + half
        return pltpu.make_async_remote_copy(
            src_ref=source, dst_ref=landed.at[block], send_sem=sem.at[t], recv_sem=near_r.at[block],
            device_id={"dp": target}, device_id_type=MESH,
        )

    def side(block, step):
        mine = full.at[block, pl.ds(pl.multiple_of(me * share, share), share), :]
        return pltpu.make_async_remote_copy(
            src_ref=mine, dst_ref=rows_out.at[section, block], send_sem=side_s.at[block, step - 1],
            recv_sem=side_r.at[section, block],
            device_id={"pipe": lax.rem(section + step, sections)}, device_id_type=MESH,
        )

    def open_block(value, block):
        m11, m21, m22 = unpack(value)
        full[block, 0:HALF, 0:HALF] = m11
        full[block, HALF:BLK, 0:HALF] = m21
        full[block, 0:HALF, HALF:BLK] = m21.T
        full[block, HALF:BLK, HALF:BLK] = m22
        for step in range(1, sections):
            side(block, step).start()
        rows_out[section, block] = full[block, pl.ds(pl.multiple_of(me * share, share), share), :]

    place = look_up(places, chip)
    for slot in range(nown):
        t = slot * chips + place

        @pl.when(t < nhalf)
        def _():
            @pl.when(chip > 0)
            def _():
                send(packed.at[slot], t, core, low, low_s).start()

            @pl.when(chip < chips - 1)
            def _():
                send(packed.at[slot], t, core, high, high_s).start()

            send(packed.at[slot], t, core, pair, pair_s).start()

    def arrived(t, half):
        send(landed.at[2 * t + half], t, half, pair, pair_s).wait_recv()

    def receive(t):
        arrived(t, core)
        source = landed.at[2 * t + core]

        @pl.when((look_up(owners, t) > chip) & (chip > 0))
        def _():
            send(source, t, core, low, low_s).start()

        @pl.when((look_up(owners, t) < chip) & (chip < chips - 1))
        def _():
            send(source, t, core, high, high_s).start()

        send(source, t, core, pair, pair_s).start()

    for slot in range(nown):
        t = slot * chips + place

        @pl.when(t < nhalf)
        def _():
            open_block(packed[slot], 2 * t + core)
            other = 2 * t + 1 - core
            arrived(t, 1 - core)
            open_block(landed[other], other)

    from_high = sorted(range(nhalf), key=lambda t: owners[t])
    from_low = sorted(range(nhalf), key=lambda t: -owners[t])
    below = sum((chip >= owner).astype(jnp.int32) for owner in owners)
    above = sum((chip <= owner).astype(jnp.int32) for owner in owners)

    @pl.loop(0, nhalf)
    def _(tick):
        i = tick + below
        t = look_up(from_high, i)
        j = tick + above
        u = look_up(from_low, j)

        @pl.when(i < nhalf)
        def _():
            receive(t)

        @pl.when(j < nhalf)
        def _():
            receive(u)

        for half in (core, 1 - core):
            for use, which in ((i < nhalf, t), (j < nhalf, u)):
                @pl.when(use)
                def _():
                    block = 2 * which + half
                    if half is not core:
                        arrived(which, half)
                    open_block(landed[block], block)

    for t in range(nhalf):
        owner = owners[t]
        source = landed.at[2 * t + core]

        @pl.when((chip > 0) & (chip <= owner))
        def _():
            send(source, t, core, low, low_s).wait_send()

        @pl.when((chip < chips - 1) & (chip >= owner))
        def _():
            send(source, t, core, high, high_s).wait_send()

        send(source, t, core, pair, pair_s).wait_send()

    @pl.loop(0, 2 * nhalf)
    def _(block):
        for step in range(1, sections):
            side(block, step).wait_send()
            source = lax.rem(section + step, sections)
            pltpu.make_async_remote_copy(
                src_ref=rows_out.at[source, block], dst_ref=rows_out.at[source, block],
                send_sem=side_s.at[block, step - 1], recv_sem=side_r.at[source, block],
                device_id={"pipe": source}, device_id_type=MESH,
            ).wait_recv()


def apply_kernel(per_step, owners, inverse, grad, rows, precond, held, slots):
    step = pl.program_id(0)
    section = lax.axis_index("pipe")
    sections, nblocks = owners.shape
    total = sections * nblocks

    @pl.when(step == 0)
    def _():
        for j in range(HOST):
            slots[j] = -1

        def place(k, used):
            hit = owners[k // nblocks, lax.rem(k, nblocks)] == section

            @pl.when(hit)
            def _():
                slots[used] = k

            return used + hit.astype(jnp.int32)

        lax.fori_loop(0, total, place, jnp.int32(0))

    for j in range(per_step):
        k = slots[step * per_step + j]
        at = jnp.maximum(k, 0)
        value = rows[at // nblocks, lax.rem(at, nblocks)]
        held[j] = jnp.where(k >= 0, value, 0.0)

    for i in range(inverse.shape[0]):
        span = slice(i * BLK, (i + 1) * BLK)
        a = inverse[i]
        b = grad[span, :]
        a_high = a.astype(BF16)
        a_low = (a - a_high.astype(F32)).astype(BF16)
        b_high = b.astype(BF16)
        b_low = (b - b_high.astype(F32)).astype(BF16)
        small = jnp.dot(a_high, b_low, preferred_element_type=F32) + jnp.dot(a_low, b_high, preferred_element_type=F32)
        precond[span, :] = jnp.dot(a_high, b_high, preferred_element_type=F32) + small


def shards(acts, grad, owner_of):
    tokens, feature_count = acts.shape[1:]
    columns = grad.shape[1]
    nblocks = feature_count // BLK
    n = lax.axis_size("dp")
    sections = lax.axis_size("pipe")
    chips = n // 2
    nhalf = nblocks // 2
    nown = -(-nhalf // chips)
    share = BLK // n
    vmem = pl.BlockSpec(memory_space=pltpu.VMEM)
    dma = pltpu.SemaphoreType.DMA

    summed = pl.pallas_call(
        functools.partial(reduce_kernel, n, nhalf, nown),
        out_shape=jax.ShapeDtypeStruct((nown, PACK, BLK), F32),
        in_specs=[vmem],
        out_specs=vmem,
        scratch_shapes=[
            pltpu.VMEM((nhalf, PACK, BLK), F32),
            pltpu.VMEM((nhalf, PACK, BLK), F32),
            pltpu.VMEM((nhalf, PACK, BLK), F32),
            pltpu.VMEM((nhalf, PACK, BLK), F32),
            pltpu.VMEM((nhalf, PACK, BLK), F32),
            dma((nhalf,)), dma((nhalf,)), dma((nhalf,)), dma((nhalf,)), dma((nhalf,)),
        ],
        compiler_params=pltpu.CompilerParams(collective_id=0, has_side_effects=True),
        name="reduce_factors",
    )(acts[0])

    packed = pl.pallas_call(
        functools.partial(invert_kernel, float(tokens * n)),
        out_shape=jax.ShapeDtypeStruct((nown, PACK, BLK), F32),
        in_specs=[vmem],
        out_specs=vmem,
        name="invert_blocks",
    )(summed)

    inverse, rows = pl.pallas_call(
        functools.partial(spread_kernel, n, sections, nhalf, nown),
        out_shape=(
            jax.ShapeDtypeStruct((nblocks, BLK, BLK), F32),
            jax.ShapeDtypeStruct((sections, nblocks, share, BLK), F32),
        ),
        in_specs=[vmem],
        out_specs=(vmem, vmem),
        scratch_shapes=[
            pltpu.VMEM((nblocks, PACK, BLK), F32),
            dma((nhalf,)), dma((nhalf,)), dma((nblocks,)), dma((nhalf,)),
            dma((nblocks, sections - 1)), dma((sections, nblocks)),
        ],
        compiler_params=pltpu.CompilerParams(collective_id=1, has_side_effects=True),
        name="spread_inverses",
    )(packed)

    group = 2 if nblocks % 2 == 0 else 1
    per_step = HOST // (nblocks // group)
    precond, held = pl.pallas_call(
        functools.partial(apply_kernel, per_step),
        grid_spec=pltpu.PrefetchScalarGridSpec(
            num_scalar_prefetch=1,
            grid=(nblocks // group,),
            in_specs=[
                pl.BlockSpec((group, BLK, BLK), lambda i, o: (i, 0, 0)),
                pl.BlockSpec((group * BLK, columns), lambda i, o: (i, 0)),
                pl.BlockSpec((sections, nblocks, share, BLK), lambda i, o: (0, 0, 0, 0), pipeline_mode=pl.Buffered(1)),
            ],
            out_specs=[
                pl.BlockSpec((group * BLK, columns), lambda i, o: (i, 0)),
                pl.BlockSpec((per_step, share, BLK), lambda i, o: (i, 0, 0)),
            ],
            scratch_shapes=[pltpu.SMEM((HOST,), jnp.int32)],
        ),
        out_shape=(
            jax.ShapeDtypeStruct((feature_count, columns), F32),
            jax.ShapeDtypeStruct((HOST, share, BLK), F32),
        ),
        compiler_params=pltpu.CompilerParams(dimension_semantics=("arbitrary",)),
        name="apply_inverses",
    )(owner_of, inverse, grad, rows)
    return precond, held[None]


def solution(mesh):
    placed = (P("pipe", "dp", None), P("pipe", "dp"), P())
    return jax.shard_map(
        shards,
        mesh=mesh,
        in_specs=placed,
        out_specs=(P("pipe", "dp"), P("pipe", None, "dp", None)),
        check_vma=False,
    )
```

profile of v0, /device:TPU:0, one launch (start us, length us, event | category | flops | bytes accessed | tf_op | source)
XLA Modules:
  0.0 81.6 jit_solution(11904422524002790308)
XLA Ops:
  0.6 26.6 %reduce_factors.1.packed = f32[2,136,256]{2,1,0:T(8,128)} custom-call(bf16[256,3072]{1,0:T(8,128)(2,1)} %bitcast.2), custom_call_target="tpu_custom_call" | custom-call | tf_op jit(solution)/shard_map/reduce_factors/pallas_call | solution.py:448
  27.2 18.1 %invert_blocks.1.packed = f32[2,136,256]{2,1,0:T(8,128)} custom-call(f32[2,136,256]{2,1,0:T(8,128)} %reduce_factors.1.packed), custom_call_target="tpu_custom_call" | custom-call | tf_op jit(solution)/shard_map/invert_blocks/pallas_call | solution.py:465
  45.3 25.7 %spread_inverses.1 = (f32[12,256,256]{2,1,0:T(8,128)}, f32[4,12,32,256]{3,2,1,0:T(8,128)}) custom-call(f32[2,136,256]{2,1,0:T(8,128)} %invert_blocks.1.packed), custom_call_target="tpu_custom_call" | custom-call | tf_op jit(solution)/shard_map/spread_inverses/pallas_call | solution.py:473
  71.0 10.5 %apply_inverses.1 = (f32[3072,512]{1,0:T(8,128)}, f32[24,32,256]{2,1,0:T(8,128)}) custom-call(s32[4,12]{1,0:T(4,128)} %owners.1, f32[12,256,256]{2,1,0:T(8,128)} %get-tuple-element.6.inverse, f32[3072,512]{1,0:T(8,128)} %grad.1, f32[4,12,32,256]{3,2,1,0:T(8,128)} %get-tuple-element.7.rows), custom_call_target="tpu_custom_call" | custom-call | tf_op jit(solution)/shard_map/apply_inverses/pallas_call | solution.py:492
where the time goes:
time: 81.9 us; the launch traced here: 81.6 us
  Pallas kernels  80.9 us (99%)
    pallas_call x1, Pallas kernels, shards(): pl.pallas_call(functools.partial(reduce_kernel, n, nhalf, nown), out_shap...  26.6 us
    pallas_call x1, Pallas kernels, shards(): pl.pallas_call(functools.partial(spread_kernel, n, sections, nhalf, nown)...  25.7 us
    pallas_call x1, Pallas kernels, shards(): pl.pallas_call(functools.partial(invert_kernel, float(tokens * n)), out_s...  18.1 us
    pallas_call x1, Pallas kernels, shards(): pl.pallas_call(functools.partial(apply_kernel, per_step), grid_spec=pltpu...  10.5 us

commit v1 on v0

v1 whole, which is shorter than its diff:
```python
import functools

import jax
import jax.numpy as jnp
from jax import lax
from jax.experimental import pallas as pl
from jax.experimental.pallas import tpu as pltpu
from jax.sharding import PartitionSpec as P

BLK = 256
HALF = BLK // 2
PACK = 2 * HALF + 8
CHUNKS = 3
CHUNK = PACK // CHUNKS
HOST = 24
UNROLL = 1
MESH = pl.DeviceIdType.MESH

damping_ratio = 0.1
F32 = jnp.float32
BF16 = jnp.bfloat16
HIGHEST = lax.Precision.HIGHEST


def square_iota():
    rows = lax.broadcasted_iota(jnp.int32, (HALF, HALF), 0)
    cols = lax.broadcasted_iota(jnp.int32, (HALF, HALF), 1)
    return rows, cols


def pack_into(ref, m11, m21, m22):
    rows, cols = square_iota()
    diag = jnp.sum(jnp.where(rows == cols, m22, 0.0), axis=0, keepdims=True)
    ref[0:HALF, :] = m21
    ref[HALF:BLK, :] = jnp.where(rows >= cols, m11, m22)
    ref[BLK:PACK, :] = jnp.broadcast_to(diag, (PACK - BLK, HALF))


def unpack(value):
    rows, cols = square_iota()
    m21 = value[0:HALF, :]
    mixed = value[HALF:BLK, :]
    diag = value[BLK : BLK + 1, :]
    turned = mixed.T
    m11 = jnp.where(rows >= cols, mixed, turned)
    m22 = jnp.where(rows < cols, mixed, jnp.where(rows == cols, diag, turned))
    return m11, m21, m22


def greet(signals):
    barrier = pltpu.get_barrier_semaphore()
    for condition, device in signals:
        if condition is None:
            pl.semaphore_signal(barrier, inc=1, device_id=device, device_id_type=MESH)
        else:
            @pl.when(condition)
            def _():
                pl.semaphore_signal(barrier, inc=1, device_id=device, device_id_type=MESH)
    peers = sum(1 if condition is None else condition.astype(jnp.int32) for condition, _ in signals)
    pl.semaphore_wait(barrier, peers)


def dot3(a, b, contract):
    return jnp.stack([
        lax.dot_general(a[i], b[i], (contract, ((), ())), precision=HIGHEST, preferred_element_type=F32)
        for i in range(a.shape[0])
    ])


def sweep_inverse(a):
    count = a.shape[0]
    panel_shape = (count, 8, HALF)
    sub = lax.broadcasted_iota(jnp.int32, panel_shape, 1)
    lane = lax.broadcasted_iota(jnp.int32, panel_shape, 2)
    all_lanes = lax.broadcasted_iota(jnp.int32, (count, HALF, HALF), 2)

    def columns_of(top, first):
        return tuple(jnp.broadcast_to(top[:, :, k : k + 1], panel_shape) for k in range(first, first + 8))

    def panel(_, state):
        a, cols = state
        cols = list(cols)
        top = a[:, 0:8, :]
        for k in range(8):
            here = cols[k]
            inv = jnp.broadcast_to(1.0 / here[:, k : k + 1, :], panel_shape)
            row = jnp.broadcast_to(top[:, k : k + 1, :], panel_shape) * inv
            at_row = sub == k
            new = jnp.where(at_row, row, top - here * row)
            edge = jnp.where(at_row, inv, -here * inv)
            top = jnp.where(lane == k, edge, new)
            for j in range(k + 1, 8):
                across = jnp.broadcast_to(cols[j][:, k : k + 1, :], panel_shape) * inv
                cols[j] = jnp.where(at_row, across, cols[j] - here * across)
        top = jnp.where(lane < 8, -top, top)
        rest = a - jnp.stack([
            lax.dot_general(a[i, 0:8, :], top[i], (((0,), (0,)), ((), ())), precision=HIGHEST, preferred_element_type=F32)
            for i in range(count)
        ])
        ahead = columns_of(rest[:, 8:16, :], 8)
        tall = jnp.concatenate([top, jnp.zeros((count, HALF - 8, HALF), F32)], axis=1)
        turned = jnp.stack([tall[i].T for i in range(count)])
        rest = jnp.where(all_lanes < 8, turned, rest)
        a = jnp.concatenate([rest[:, 8:, :], top], axis=1)
        return pltpu.roll(a, HALF - 8, 2), ahead

    return -lax.fori_loop(0, HALF // 8, panel, (a, columns_of(a[:, 0:8, :], 0)), unroll=UNROLL)[0]


def invert_parts(values, tokens):
    rows, cols = square_iota()
    parts = [unpack(value / tokens) for value in values]
    m11 = jnp.stack([p[0] for p in parts])
    m21 = jnp.stack([p[1] for p in parts])
    m22 = jnp.stack([p[2] for p in parts])
    eye = rows == cols
    trace = jnp.sum(jnp.where(eye, m11 + m22, 0.0), axis=(1, 2), keepdims=True)
    damping = jnp.where(eye, damping_ratio * trace / BLK, 0.0)
    x11 = sweep_inverse(m11 + damping)
    g = dot3(m21, x11, ((1,), (0,)))
    schur = m22 + damping - dot3(g, m21, ((1,), (1,)))
    y = sweep_inverse(schur)
    b21 = -dot3(y, g, ((1,), (0,)))
    b11 = x11 - dot3(g, b21, ((0,), (0,)))
    return b11, b21, y


def solve_kernel(n, sections, nblocks, tokens, acts, grad, precond, rows_out, acts_v, grad_v, theirs, mine, from_pair,
                 inbound, landed, full, acts_s, grad_s, pair_s, pair_r, sum_s, sum_r, line_s, swap_s, near_r,
                 side_s, side_r):
    chips = n // 2
    nhalf = nblocks // 2
    nown = -(-nhalf // 2)
    share = BLK // n
    me = lax.axis_index("dp")
    section = lax.axis_index("pipe")
    core = lax.rem(me, 2)
    chip = me // 2
    pair = me + 1 - 2 * core
    low = (jnp.maximum(chip - 1, 0)) * 2 + core
    high = (jnp.minimum(chip + 1, chips - 1)) * 2 + core
    first = chip == 0
    last = chip == chips - 1
    is_last = last.astype(jnp.int32)

    def acts_copy(t):
        span = pl.ds(pl.multiple_of(t * 2 * BLK, 2 * BLK), 2 * BLK)
        return pltpu.make_async_copy(acts.at[:, span], acts_v.at[:, span], acts_s.at[t])

    def turn_of(p):
        natural = p
        up_first = jnp.where(p < nhalf // 2, 2 * p + 1, 2 * (p - nhalf // 2))
        down_first = jnp.where(p < nown, 2 * p, 2 * (p - nown) + 1)
        return jnp.where(first, up_first, jnp.where(last, down_first, natural))

    for p in range(nhalf):
        acts_copy(turn_of(p)).start()
    grad_copy = pltpu.make_async_copy(grad, grad_v, grad_s)
    grad_copy.start()

    greet(
        [(None, {"dp": pair}), (chip > 0, {"dp": low}), (chip < chips - 1, {"dp": high})]
        + [(None, {"pipe": lax.rem(section + step, sections)}) for step in range(1, sections)]
    )

    def partial(block, ref):
        x = acts_v[:, pl.ds(pl.multiple_of(block * BLK, BLK), BLK)]
        whole = lax.dot_general(x, x, (((0,), (0,)), ((), ())), preferred_element_type=F32)
        pack_into(ref, whole[0:HALF, 0:HALF], whole[HALF:BLK, 0:HALF], whole[HALF:BLK, HALF:BLK])

    def pair_copy(t):
        return pltpu.make_async_remote_copy(
            src_ref=theirs.at[t], dst_ref=from_pair.at[t], send_sem=pair_s.at[t], recv_sem=pair_r.at[t],
            device_id={"dp": pair}, device_id_type=MESH,
        )

    def fold_pair(t):
        pair_copy(t).wait()
        mine[t] = mine[t] + from_pair[t]

    def piece(k):
        return pl.ds(k * CHUNK, CHUNK)

    def sum_copy(t, k, target):
        return pltpu.make_async_remote_copy(
            src_ref=mine.at[t, piece(k)], dst_ref=inbound.at[t, piece(k)], send_sem=sum_s.at[t, k],
            recv_sem=sum_r.at[t, k], device_id={"dp": target}, device_id_type=MESH,
        )

    def pass_sum(t, k, heads, target):
        @pl.when(jnp.logical_not(heads))
        def _():
            sum_copy(t, k, target).wait_recv()
            mine[t, piece(k)] = mine[t, piece(k)] + inbound[t, piece(k)]

        sum_copy(t, k, target).start()

    @pl.loop(0, nown + chips)
    def _(tick):
        for p in (2 * tick, 2 * tick + 1):
            @pl.when(p < nhalf)
            def _():
                t = turn_of(p)
                acts_copy(t).wait()
                partial(2 * t + 1 - core, theirs.at[t])
                pair_copy(t).start()
                partial(2 * t + core, mine.at[t])

        i = tick - 1 - chip
        t = 2 * i + 1
        rising = (i >= 0) & (t < nhalf) & jnp.logical_not(last)
        j = tick - 1 - (chips - 1 - chip)
        u = 2 * j
        falling = (j >= 0) & (u < nhalf) & jnp.logical_not(first)

        @pl.when(rising)
        def _():
            fold_pair(t)

        @pl.when(falling)
        def _():
            fold_pair(u)

        for k in range(CHUNKS):
            @pl.when(rising)
            def _():
                pass_sum(t, k, first, high)

            @pl.when(falling)
            def _():
                pass_sum(u, k, last, low)

    def close_sum(t):
        fold_pair(t)
        for k in range(CHUNKS):
            sum_copy(t, k, low).wait_recv()
        return mine[t] + inbound[t]

    def invert(slots):
        own = [2 * slot + is_last for slot in slots]
        b11, b21, b22 = invert_parts([close_sum(t) for t in own], tokens)
        for i, t in enumerate(own):
            pack_into(landed.at[2 * t + core], b11[i], b21[i], b22[i])

    def send(t, half, k, target, sem):
        block = 2 * t + half
        return pltpu.make_async_remote_copy(
            src_ref=landed.at[block, piece(k)], dst_ref=landed.at[block, piece(k)], send_sem=sem.at[t, k],
            recv_sem=near_r.at[block, k], device_id={"dp": target}, device_id_type=MESH,
        )

    def flow(t, k, owned, ends, target):
        @pl.when(jnp.logical_not(owned))
        def _():
            send(t, core, k, pair, swap_s).wait_recv()

        @pl.when(jnp.logical_not(ends))
        def _():
            send(t, core, k, target, line_s).start()

        send(t, core, k, pair, swap_s).start()

    def side(block, step):
        mine_rows = full.at[block, pl.ds(pl.multiple_of(me * share, share), share), :]
        return pltpu.make_async_remote_copy(
            src_ref=mine_rows, dst_ref=rows_out.at[section, block], send_sem=side_s.at[block, step - 1],
            recv_sem=side_r.at[section, block],
            device_id={"pipe": lax.rem(section + step, sections)}, device_id_type=MESH,
        )

    def open_block(block):
        m11, m21, m22 = unpack(landed[block])
        full[block, 0:HALF, 0:HALF] = m11
        full[block, HALF:BLK, 0:HALF] = m21
        full[block, 0:HALF, HALF:BLK] = m21.T
        full[block, HALF:BLK, HALF:BLK] = m22
        for step in range(1, sections):
            side(block, step).start()
        rows_out[section, block] = full[block, pl.ds(pl.multiple_of(me * share, share), share), :]

    def open_other(t):
        for k in range(CHUNKS):
            send(t, 1 - core, k, pair, swap_s).wait_recv()
        open_block(2 * t + 1 - core)

    def product(block):
        span = pl.ds(pl.multiple_of(block * BLK, BLK), BLK)
        a = full[block]
        b = grad_v[span, :]
        a_high = a.astype(BF16)
        a_low = (a - a_high.astype(F32)).astype(BF16)
        b_high = b.astype(BF16)
        b_low = (b - b_high.astype(F32)).astype(BF16)
        small = jnp.dot(a_high, b_low, preferred_element_type=F32) + jnp.dot(a_low, b_high, preferred_element_type=F32)
        precond[span, :] = jnp.dot(a_high, b_high, preferred_element_type=F32) + small

    def both_products(t):
        @pl.loop(0, 2)
        def _(half):
            product(2 * t + half)

    @pl.loop(0, nown + chips)
    def _(tick):
        i = tick - chip
        t = 2 * i
        rising = (i >= 0) & (t < nhalf)
        j = tick - (chips - 1 - chip)
        u = 2 * j + 1
        falling = (j >= 0) & (u < nhalf)
        rose = (i >= 1) & (t - 2 < nhalf)
        fell = (j >= 1) & (u - 2 < nhalf)

        @pl.when((tick == 0) & (first | last))
        def _():
            invert([0])

        @pl.when((tick == 1) & (first | last))
        def _():
            invert(list(range(1, nown)))

        for k in range(CHUNKS):
            @pl.when(rising)
            def _():
                flow(t, k, first, last, high)

            @pl.when(falling)
            def _():
                flow(u, k, last, first, low)

            if k == 0:
                @pl.when(rose)
                def _():
                    open_other(t - 2)

                @pl.when(fell)
                def _():
                    open_other(u - 2)

                @pl.when(tick == 1)
                def _():
                    grad_copy.wait()

            if k == 1:
                @pl.when(rose)
                def _():
                    both_products(t - 2)

            if k == 2:
                @pl.when(rising)
                def _():
                    open_block(2 * t + core)

                @pl.when(falling)
                def _():
                    open_block(2 * u + core)

                @pl.when(fell)
                def _():
                    both_products(u - 2)

    @pl.loop(0, nhalf)
    def _(t):
        odd = lax.rem(t, 2) == 1
        sends_sum = jnp.where(odd, jnp.logical_not(last), jnp.logical_not(first))
        sends_inverse = jnp.where(odd, jnp.logical_not(first), jnp.logical_not(last))
        for k in range(CHUNKS):
            @pl.when(sends_sum)
            def _():
                sum_copy(t, k, low).wait_send()

            @pl.when(sends_inverse)
            def _():
                send(t, core, k, low, line_s).wait_send()

            send(t, core, k, pair, swap_s).wait_send()

    @pl.loop(0, nblocks)
    def _(block):
        for step in range(1, sections):
            side(block, step).wait_send()
            source = lax.rem(section + step, sections)
            pltpu.make_async_remote_copy(
                src_ref=rows_out.at[source, block], dst_ref=rows_out.at[source, block],
                send_sem=side_s.at[block, step - 1], recv_sem=side_r.at[source, block],
                device_id={"pipe": source}, device_id_type=MESH,
            ).wait_recv()


def emit_kernel(owners, values, rows, precond, held, slots, zeros, copy_s, held_s):
    section = lax.axis_index("pipe")
    sections, nblocks = owners.shape
    total = sections * nblocks
    zeros[...] = jnp.zeros_like(zeros)

    def precond_copy(b):
        span = pl.ds(pl.multiple_of(b * BLK, BLK), BLK)
        return pltpu.make_async_copy(values.at[span, :], precond.at[span, :], copy_s.at[b])

    for b in range(nblocks):
        precond_copy(b).start()

    for j in range(HOST):
        slots[j] = -1

    def place(k, used):
        hit = owners[k // nblocks, lax.rem(k, nblocks)] == section

        @pl.when(hit)
        def _():
            slots[used] = k

        return used + hit.astype(jnp.int32)

    lax.fori_loop(0, total, place, jnp.int32(0))

    @pl.loop(0, HOST)
    def _(j):
        k = slots[j]

        @pl.when(k >= 0)
        def _():
            pltpu.make_async_copy(rows.at[k // nblocks, lax.rem(k, nblocks)], held.at[j], held_s.at[j]).start()

        @pl.when(k < 0)
        def _():
            pltpu.make_async_copy(zeros, held.at[j], held_s.at[j]).start()

    @pl.loop(0, HOST)
    def _(j):
        pltpu.make_async_copy(zeros, held.at[j], held_s.at[j]).wait()

    for b in range(nblocks):
        precond_copy(b).wait()


def shards(acts, grad, owner_of):
    tokens, feature_count = acts.shape[1:]
    columns = grad.shape[1]
    nblocks = feature_count // BLK
    n = lax.axis_size("dp")
    sections = lax.axis_size("pipe")
    nhalf = nblocks // 2
    share = BLK // n
    vmem = pl.BlockSpec(memory_space=pltpu.VMEM)
    hbm = pl.BlockSpec(memory_space=pltpu.HBM)
    smem = pl.BlockSpec(memory_space=pltpu.SMEM)
    dma = pltpu.SemaphoreType.DMA

    values, rows = pl.pallas_call(
        functools.partial(solve_kernel, n, sections, nblocks, float(tokens * n)),
        out_shape=(
            pltpu.VMEM((feature_count, columns), F32),
            pltpu.VMEM((sections, nblocks, share, BLK), F32),
        ),
        in_specs=[hbm, hbm],
        out_specs=(vmem, vmem),
        scratch_shapes=[
            pltpu.VMEM((tokens, feature_count), BF16),
            pltpu.VMEM((feature_count, columns), F32),
            pltpu.VMEM((nhalf, PACK, HALF), F32),
            pltpu.VMEM((nhalf, PACK, HALF), F32),
            pltpu.VMEM((nhalf, PACK, HALF), F32),
            pltpu.VMEM((nhalf, PACK, HALF), F32),
            pltpu.VMEM((nblocks, PACK, HALF), F32),
            pltpu.VMEM((nblocks, BLK, BLK), F32),
            dma((nhalf,)), dma, dma((nhalf,)), dma((nhalf,)), dma((nhalf, CHUNKS)), dma((nhalf, CHUNKS)),
            dma((nhalf, CHUNKS)), dma((nhalf, CHUNKS)), dma((nblocks, CHUNKS)),
            dma((nblocks, sections - 1)), dma((sections, nblocks)),
        ],
        compiler_params=pltpu.CompilerParams(collective_id=0, has_side_effects=True, vmem_limit_bytes=36 * 2**20),
        name="solve_blocks",
    )(pltpu.with_memory_space_constraint(acts[0], pltpu.HBM), pltpu.with_memory_space_constraint(grad, pltpu.HBM))

    precond, held = pl.pallas_call(
        emit_kernel,
        in_specs=[smem, vmem, vmem],
        out_specs=(hbm, hbm),
        out_shape=(
            jax.ShapeDtypeStruct((feature_count, columns), F32),
            jax.ShapeDtypeStruct((HOST, share, BLK), F32),
        ),
        scratch_shapes=[pltpu.SMEM((HOST,), jnp.int32), pltpu.VMEM((share, BLK), F32), dma((nblocks,)), dma((HOST,))],
        compiler_params=pltpu.CompilerParams(vmem_limit_bytes=16 * 2**20),
        name="emit_outputs",
    )(owner_of, values, rows)
    return precond, held[None]


def solution(mesh):
    placed = (P("pipe", "dp", None), P("pipe", "dp"), P())
    return jax.shard_map(
        shards,
        mesh=mesh,
        in_specs=placed,
        out_specs=(P("pipe", "dp"), P("pipe", None, "dp", None)),
        check_vma=False,
    )
```

time: 81.9 us -> 75.1 us (0.917)
  Pallas kernels: 80.9 us -> 74.3 us
    pallas_call x4 -> x2, Pallas kernels: 80.9 us -> 74.3 us  [the longest x1 70.6 us: shards(): pl.pallas_call(functools.partial(solve_kernel, n, sections, nblocks, floa...]
where the time goes in v1:
time: 75.1 us; the launch traced here: 75 us
  Pallas kernels  74.3 us (99%)
    pallas_call x1, Pallas kernels, shards(): pl.pallas_call(functools.partial(solve_kernel, n, sections, nblocks, floa...  70.6 us
    pallas_call x1, Pallas kernels, shards(): pl.pallas_call(emit_kernel, in_specs=[smem, vmem, vmem], out_specs=(hbm,...  3.75 us

profile of v1, /device:TPU:0, one launch (start us, length us, event | category | flops | bytes accessed | tf_op | source)
XLA Modules:
  0.0 75.0 jit_solution(9315955361683368333)
XLA Ops:
  0.6 0.0 copy-start
  0.6 70.6 %solve_blocks.1 = (f32[3072,512]{1,0:T(8,128)S(1)}, f32[4,12,32,256]{3,2,1,0:T(8,128)S(1)}) custom-call(bf16[256,3072]{1,0:T(8,128)(2,1)} %bitcast.2, f32[3072,512]{1,0:T(8,128)} %grad.1), custom_call_target="tpu_custom_call" | custom-call | tf_op jit(solution)/shard_map/solve_blocks/pallas_call | solution.py:449
  71.2 0.0 copy-done
  71.2 3.7 %emit_outputs.1 = (f32[3072,512]{1,0:T(8,128)}, f32[24,32,256]{2,1,0:T(8,128)}) custom-call(s32[4,12]{1,0:T(4,128)S(1)} %copy-done, f32[3072,512]{1,0:T(8,128)S(1)} %get-tuple-element.6.values, f32[4,12,32,256]{3,2,1,0:T(8,128)S(1)} %get-tuple-element.7.rows), custom_call_target="tpu_custom_call" | custom-call | tf_op jit(solution)/shard_map/emit_outputs/pallas_call | solution.py:474
Async XLA Ops:
  0.6 70.6 %copy-start = (s32[4,12]{1,0:T(4,128)S(1)}, s32[4,12]{1,0:T(4,128)}, u32[]{:S(2)}) copy-start(s32[4,12]{1,0:T(4,128)} %owners.1) | copy-start | bytes 580

commit v2 on v1

--- a/solution.py
+++ b/solution.py
@@ -13,6 +13,7 @@
 CHUNKS = 3
 CHUNK = PACK // CHUNKS
 HOST = 24
+PANEL = 16
 UNROLL = 1
 MESH = pl.DeviceIdType.MESH
 
@@ -60,69 +61,107 @@
     pl.semaphore_wait(barrier, peers)
 
 
-def dot3(a, b, contract):
-    return jnp.stack([
-        lax.dot_general(a[i], b[i], (contract, ((), ())), precision=HIGHEST, preferred_element_type=F32)
-        for i in range(a.shape[0])
-    ])
-
-
-def sweep_inverse(a):
-    count = a.shape[0]
-    panel_shape = (count, 8, HALF)
-    sub = lax.broadcasted_iota(jnp.int32, panel_shape, 1)
-    lane = lax.broadcasted_iota(jnp.int32, panel_shape, 2)
-    all_lanes = lax.broadcasted_iota(jnp.int32, (count, HALF, HALF), 2)
-
-    def columns_of(top, first):
-        return tuple(jnp.broadcast_to(top[:, :, k : k + 1], panel_shape) for k in range(first, first + 8))
+def thirds(x):
+    high = x.astype(BF16)
+    rest = x - high.astype(F32)
+    mid = rest.astype(BF16)
+    return high, mid, (rest - mid.astype(F32)).astype(BF16)
+
+
+def wide_dot(left, right):
+    lh, lm, ll = thirds(left)
+    rh, rm, rl = thirds(right)
+    return lax.dot_general(
+        jnp.concatenate([lh, lh, lm, lh, lm, ll], axis=0), jnp.concatenate([rh, rm, rh, rl, rm, rh], axis=0),
+        (((0,), (0,)), ((), ())), preferred_element_type=F32,
+    )
+
+
+def sweep_inverse(blocks):
+    groups = PANEL // 8
+    sub = lax.broadcasted_iota(jnp.int32, (8, HALF), 0)
+    lane = lax.broadcasted_iota(jnp.int32, (8, HALF), 1)
+    all_lanes = lax.broadcasted_iota(jnp.int32, (HALF, HALF), 1)
+
+    def splat(value, row):
+        return jnp.broadcast_to(value[row : row + 1, :], (8, HALF))
+
+    def columns_of(rows, at):
+        return tuple(
+            tuple(jnp.broadcast_to(rows[8 * g : 8 * g + 8, at + j : at + j + 1], (8, HALF)) for g in range(groups))
+            for j in range(PANEL)
+        )
+
+    def pivots(a, cols):
+        cols = [list(c) for c in cols]
+        top = [jnp.where(lane < PANEL, (lane == sub + 8 * g).astype(F32), a[8 * g : 8 * g + 8, :]) for g in range(groups)]
+        for k in range(PANEL):
+            at, row = k // 8, k % 8
+            here = cols[k]
+            inv = 1.0 / splat(here[at], row)
+            hit = sub == row
+            scaled = [jnp.where(hit, -inv, here[g] * inv) if g == at else here[g] * inv for g in range(groups)]
+
+            def eliminate(target):
+                lead = splat(target[at], row)
+                return [
+                    (jnp.where(hit, 0.0, target[g]) if g == at else target[g]) - scaled[g] * lead for g in range(groups)
+                ]
+
+            for j in range(k + 1, PANEL):
+                cols[j] = eliminate(cols[j])
+            top = eliminate(top)
+        return jnp.concatenate([jnp.where(lane < PANEL, -t, t) for t in top], axis=0)
+
+    def update(a, top, near):
+        ahead = [jnp.where(lane < PANEL, 0.0, a[PANEL + 8 * g : PANEL + 8 * g + 8, :]) for g in range(groups)]
+        for g in range(groups):
+            terms = [near[k][g] * splat(top[8 * (k // 8) : 8 * (k // 8) + 8, :], k % 8) for k in range(PANEL)]
+            while len(terms) > 1:
+                terms = [terms[i] + terms[i + 1] for i in range(0, len(terms), 2)]
+            ahead[g] = ahead[g] - terms[0]
+        ahead = jnp.concatenate(ahead, axis=0)
+        below = jnp.where(all_lanes[2 * PANEL :, :] < PANEL, 0.0, a[2 * PANEL :, :]) - wide_dot(a[0:PANEL, 2 * PANEL :], top)
+        cols = columns_of(ahead, PANEL)
+        return pltpu.roll(jnp.concatenate([ahead, below, top], axis=0), HALF - PANEL, 1), cols
 
     def panel(_, state):
-        a, cols = state
-        cols = list(cols)
-        top = a[:, 0:8, :]
-        for k in range(8):
-            here = cols[k]
-            inv = jnp.broadcast_to(1.0 / here[:, k : k + 1, :], panel_shape)
-            row = jnp.broadcast_to(top[:, k : k + 1, :], panel_shape) * inv
-            at_row = sub == k
-            new = jnp.where(at_row, row, top - here * row)
-            edge = jnp.where(at_row, inv, -here * inv)
-            top = jnp.where(lane == k, edge, new)
-            for j in range(k + 1, 8):
-                across = jnp.broadcast_to(cols[j][:, k : k + 1, :], panel_shape) * inv
-                cols[j] = jnp.where(at_row, across, cols[j] - here * across)
-        top = jnp.where(lane < 8, -top, top)
-        rest = a - jnp.stack([
-            lax.dot_general(a[i, 0:8, :], top[i], (((0,), (0,)), ((), ())), precision=HIGHEST, preferred_element_type=F32)
-            for i in range(count)
-        ])
-        ahead = columns_of(rest[:, 8:16, :], 8)
-        tall = jnp.concatenate([top, jnp.zeros((count, HALF - 8, HALF), F32)], axis=1)
-        turned = jnp.stack([tall[i].T for i in range(count)])
-        rest = jnp.where(all_lanes < 8, turned, rest)
-        a = jnp.concatenate([rest[:, 8:, :], top], axis=1)
-        return pltpu.roll(a, HALF - 8, 2), ahead
-
-    return -lax.fori_loop(0, HALF // 8, panel, (a, columns_of(a[:, 0:8, :], 0)), unroll=UNROLL)[0]
+        out = []
+        for a, cols in state:
+            near = columns_of(a[PANEL : 2 * PANEL, :], 0)
+            top = pivots(a, cols)
+            out.append(update(a, top, near))
+        return tuple(out)
+
+    start = tuple((a, columns_of(a[0:PANEL, :], 0)) for a in blocks)
+    return [-a for a, _ in lax.fori_loop(0, HALF // PANEL, panel, start, unroll=UNROLL)]
+
+
+def high_dot(a, b, contract):
+    return lax.dot_general(a, b, (contract, ((), ())), precision=HIGHEST, preferred_element_type=F32)
+
+
+def invert_dense(m11, m21, m22):
+    count=len(m11)
+    x11 = sweep_inverse(m11)
+    g = [high_dot(m21[i], x11[i], ((1,), (0,))) for i in range(count)]
+    y = sweep_inverse([m22[i] - high_dot(g[i], m21[i], ((1,), (1,))) for i in range(count)])
+    b21 = [-high_dot(y[i], g[i], ((1,), (0,))) for i in range(count)]
+    b11 = [x11[i] - high_dot(g[i], b21[i], ((0,), (0,))) for i in range(count)]
+    return b11, b21, y
 
 
 def invert_parts(values, tokens):
     rows, cols = square_iota()
-    parts = [unpack(value / tokens) for value in values]
-    m11 = jnp.stack([p[0] for p in parts])
-    m21 = jnp.stack([p[1] for p in parts])
-    m22 = jnp.stack([p[2] for p in parts])
     eye = rows == cols
-    trace = jnp.sum(jnp.where(eye, m11 + m22, 0.0), axis=(1, 2), keepdims=True)
-    damping = jnp.where(eye, damping_ratio * trace / BLK, 0.0)
-    x11 = sweep_inverse(m11 + damping)
-    g = dot3(m21, x11, ((1,), (0,)))
-    schur = m22 + damping - dot3(g, m21, ((1,), (1,)))
-    y = sweep_inverse(schur)
-    b21 = -dot3(y, g, ((1,), (0,)))
-    b11 = x11 - dot3(g, b21, ((0,), (0,)))
-    return b11, b21, y
+    m11, m21, m22 = [], [], []
+    for value in values:
+        p11, p21, p22 = unpack(value / tokens)
+        damping = damping_ratio * jnp.sum(jnp.where(eye, p11 + p22, 0.0), axis=(0, 1), keepdims=True) / BLK
+        m11.append(p11 + jnp.where(eye, damping, 0.0))
+        m21.append(p21)
+        m22.append(p22 + jnp.where(eye, damping, 0.0))
+    return invert_dense(m11, m21, m22)
 
 
 def solve_kernel(n, sections, nblocks, tokens, acts, grad, precond, rows_out, acts_v, grad_v, theirs, mine, from_pair,

time: 75.1 us -> 65.3 us (0.87)
  Pallas kernels: 74.3 us -> 64.5 us
    pallas_call x1, Pallas kernels: 70.6 us -> 60.7 us  [shards(): pl.pallas_call(functools.partial(solve_kernel, n, sections, nblocks, floa...]
where the time goes in v2:
time: 65.3 us; the launch traced here: 65.1 us
  Pallas kernels  64.5 us (99%)
    pallas_call x1, Pallas kernels, shards(): pl.pallas_call(functools.partial(solve_kernel, n, sections, nblocks, floa...  60.7 us
    pallas_call x1, Pallas kernels, shards(): pl.pallas_call(emit_kernel, in_specs=[smem, vmem, vmem], out_specs=(hbm,...  3.75 us

profile of v2, /device:TPU:0, one launch (start us, length us, event | category | flops | bytes accessed | tf_op | source)
XLA Modules:
  0.0 65.1 jit_solution(1932542012344888901)
XLA Ops:
  0.6 0.0 copy-start
  0.6 60.7 %solve_blocks.1 = (f32[3072,512]{1,0:T(8,128)S(1)}, f32[4,12,32,256]{3,2,1,0:T(8,128)S(1)}) custom-call(bf16[256,3072]{1,0:T(8,128)(2,1)} %bitcast.2, f32[3072,512]{1,0:T(8,128)} %grad.1), custom_call_target="tpu_custom_call" | custom-call | tf_op jit(solution)/shard_map/solve_blocks/pallas_call | solution.py:488
  61.4 0.0 copy-done
  61.4 3.7 %emit_outputs.1 = (f32[3072,512]{1,0:T(8,128)}, f32[24,32,256]{2,1,0:T(8,128)}) custom-call(s32[4,12]{1,0:T(4,128)S(1)} %copy-done, f32[3072,512]{1,0:T(8,128)S(1)} %get-tuple-element.6.values, f32[4,12,32,256]{3,2,1,0:T(8,128)S(1)} %get-tuple-element.7.rows), custom_call_target="tpu_custom_call" | custom-call | tf_op jit(solution)/shard_map/emit_outputs/pallas_call | solution.py:513
Async XLA Ops:
  0.6 60.7 %copy-start = (s32[4,12]{1,0:T(4,128)S(1)}, s32[4,12]{1,0:T(4,128)}, u32[]{:S(2)}) copy-start(s32[4,12]{1,0:T(4,128)} %owners.1) | copy-start | bytes 580

commit v3 on v2

--- a/solution.py
+++ b/solution.py
@@ -10,8 +10,8 @@
 BLK = 256
 HALF = BLK // 2
 PACK = 2 * HALF + 8
-CHUNKS = 3
-CHUNK = PACK // CHUNKS
+PIECES = tuple((88 * i, 88) for i in range(3))
+CHUNKS = len(PIECES)
 HOST = 24
 PANEL = 16
 UNROLL = 1
@@ -58,7 +58,7 @@
             def _():
                 pl.semaphore_signal(barrier, inc=1, device_id=device, device_id_type=MESH)
     peers = sum(1 if condition is None else condition.astype(jnp.int32) for condition, _ in signals)
-    pl.semaphore_wait(barrier, peers)
+    return lambda: pl.semaphore_wait(barrier, peers)
 
 
 def thirds(x):
@@ -69,11 +69,15 @@
 
 
 def wide_dot(left, right):
-    lh, lm, ll = thirds(left)
-    rh, rm, rl = thirds(right)
+    lefts, rights = [], []
+    for l, r in zip(left, right):
+        lh, lm, ll = thirds(l)
+        rh, rm, rl = thirds(r)
+        lefts += [lh, lh, lm, lh, lm, ll]
+        rights += [rh, rm, rh, rl, rm, rh]
     return lax.dot_general(
-        jnp.concatenate([lh, lh, lm, lh, lm, ll], axis=0), jnp.concatenate([rh, rm, rh, rl, rm, rh], axis=0),
-        (((0,), (0,)), ((), ())), preferred_element_type=F32,
+        jnp.concatenate(lefts, axis=0), jnp.concatenate(rights, axis=0), (((0,), (0,)), ((), ())),
+        preferred_element_type=F32,
     )
 
 
@@ -121,7 +125,7 @@
                 terms = [terms[i] + terms[i + 1] for i in range(0, len(terms), 2)]
             ahead[g] = ahead[g] - terms[0]
         ahead = jnp.concatenate(ahead, axis=0)
-        below = jnp.where(all_lanes[2 * PANEL :, :] < PANEL, 0.0, a[2 * PANEL :, :]) - wide_dot(a[0:PANEL, 2 * PANEL :], top)
+        below = jnp.where(all_lanes[2 * PANEL :, :] < PANEL, 0.0, a[2 * PANEL :, :]) - wide_dot([a[0:PANEL, 2 * PANEL :]], [top])
         cols = columns_of(ahead, PANEL)
         return pltpu.roll(jnp.concatenate([ahead, below, top], axis=0), HALF - PANEL, 1), cols
 
@@ -137,21 +141,119 @@
     return [-a for a, _ in lax.fori_loop(0, HALF // PANEL, panel, start, unroll=UNROLL)]
 
 
+def sweep_pair(first, second, store):
+    groups = PANEL // 8
+    side = HALF // 2
+    per_side = side // PANEL
+    steps = HALF // PANEL
+    sub = lax.broadcasted_iota(jnp.int32, (8, HALF), 0)
+    lane = lax.broadcasted_iota(jnp.int32, (8, HALF), 1)
+    shift = jnp.where(lane < side, 0, side)
+    at_lane = lane - shift
+    left_rows = lax.broadcasted_iota(jnp.int32, (PANEL, HALF), 1) < side
+    wide_lane = lax.broadcasted_iota(jnp.int32, (HALF, HALF), 1)
+    left_wide = wide_lane < side
+    wide_at = jnp.where(left_wide, wide_lane, wide_lane - side)
+
+    def splat(value, row):
+        return jnp.broadcast_to(value[row : row + 1, :], (8, HALF))
+
+    def columns_at(rows, p):
+        source = jnp.where(p % (2 * per_side) < per_side, rows[0], rows[1])
+        base = lax.rem(p, per_side) * PANEL
+        return tuple(
+            tuple(
+                jnp.take_along_axis(source[8 * g : 8 * g + 8, :], shift + (base + j), axis=1, mode="promise_in_bounds")
+                for g in range(groups)
+            )
+            for j in range(PANEL)
+        )
+
+    def inside(lanes, v, p):
+        start = p * PANEL - v * side
+        return (lanes >= start) & (lanes < start + PANEL)
+
+    def pivots(rows, cols, p):
+        cols = [list(c) for c in cols]
+        tops = []
+        for v in range(2):
+            start = p * PANEL - v * side
+            tops.append([
+                jnp.where(inside(at_lane, v, p), (at_lane == sub + (start + 8 * g)).astype(F32), rows[v][8 * g : 8 * g + 8, :])
+                for g in range(groups)
+            ])
+        for k in range(PANEL):
+            at, row = k // 8, k % 8
+            here = cols[k]
+            inv = 1.0 / splat(here[at], row)
+            hit = sub == row
+            scaled = [jnp.where(hit, -inv, here[g] * inv) if g == at else here[g] * inv for g in range(groups)]
+
+            def eliminate(target):
+                lead = splat(target[at], row)
+                return [
+                    (jnp.where(hit, 0.0, target[g]) if g == at else target[g]) - scaled[g] * lead for g in range(groups)
+                ]
+
+            for j in range(k + 1, PANEL):
+                cols[j] = eliminate(cols[j])
+            tops = [eliminate(top) for top in tops]
+        return [
+            jnp.concatenate([jnp.where(inside(at_lane, v, p), -t, t) for t in tops[v]], axis=0) for v in range(2)
+        ]
+
+    def panel(p, state):
+        rows, cols = state
+        following = pl.ds(pl.multiple_of(jnp.minimum(p + 1, steps - 1) * PANEL, PANEL), PANEL)
+        after = [store[v, following, :] for v in range(2)]
+        near = columns_at(after, p)
+        tops = pivots(rows, cols, p)
+        ahead = []
+        for v in range(2):
+            parts = []
+            for g in range(groups):
+                terms = [near[k][g] * splat(tops[v][8 * (k // 8) : 8 * (k // 8) + 8, :], k % 8) for k in range(PANEL)]
+                while len(terms) > 1:
+                    terms = [terms[i] + terms[i + 1] for i in range(0, len(terms), 2)]
+                parts.append(jnp.where(inside(at_lane, v, p), 0.0, after[v][8 * g : 8 * g + 8, :]) - terms[0])
+            ahead.append(jnp.concatenate(parts, axis=0))
+        one = jnp.where(left_rows, rows[0], pltpu.roll(rows[1], side, 1))
+        two = jnp.where(left_rows, pltpu.roll(rows[0], side, 1), rows[1])
+        for v in range(2):
+            change = wide_dot([one, two], [jnp.where(left_rows, tops[v], 0.0), jnp.where(left_rows, 0.0, tops[v])])
+            store[v] = jnp.where(inside(wide_at, v, p), 0.0, store[v]) - change
+            store[v, pl.ds(pl.multiple_of(p * PANEL, PANEL), PANEL), :] = tops[v]
+        return ahead, columns_at(ahead, p + 1)
+
+    store[0] = jnp.where(left_wide, first, pltpu.roll(second, side, 1))
+    store[1] = jnp.where(left_wide, pltpu.roll(first, side, 1), second)
+    rows = [store[v, 0:PANEL, :] for v in range(2)]
+    lax.fori_loop(0, steps, panel, (rows, columns_at(rows, 0)), unroll=UNROLL)
+    return [
+        -jnp.where(left_wide, store[0], pltpu.roll(store[1], side, 1)),
+        -jnp.where(left_wide, pltpu.roll(store[0], side, 1), store[1]),
+    ]
+
+
 def high_dot(a, b, contract):
     return lax.dot_general(a, b, (contract, ((), ())), precision=HIGHEST, preferred_element_type=F32)
 
 
-def invert_dense(m11, m21, m22):
-    count=len(m11)
-    x11 = sweep_inverse(m11)
+def invert_dense(m11, m21, m22, store):
+    count = len(m11)
+
+    def sweep(blocks):
+        return sweep_pair(*blocks, store) if count == 2 else sweep_inverse(blocks)
+
+    x11 = sweep(m11)
     g = [high_dot(m21[i], x11[i], ((1,), (0,))) for i in range(count)]
-    y = sweep_inverse([m22[i] - high_dot(g[i], m21[i], ((1,), (1,))) for i in range(count)])
+    y = sweep([m22[i] - high_dot(g[i], m21[i], ((1,), (1,))) for i in range(count)])
     b21 = [-high_dot(y[i], g[i], ((1,), (0,))) for i in range(count)]
     b11 = [x11[i] - high_dot(g[i], b21[i], ((0,), (0,))) for i in range(count)]
     return b11, b21, y
 
 
-def invert_parts(values, tokens):
+def invert_parts(values, tokens, store):
     rows, cols = square_iota()
     eye = rows == cols
     m11, m21, m22 = [], [], []
@@ -161,11 +263,11 @@
         m11.append(p11 + jnp.where(eye, damping, 0.0))
         m21.append(p21)
         m22.append(p22 + jnp.where(eye, damping, 0.0))
-    return invert_dense(m11, m21, m22)
+    return invert_dense(m11, m21, m22, store)
 
 
 def solve_kernel(n, sections, nblocks, tokens, acts, grad, precond, rows_out, acts_v, grad_v, theirs, mine, from_pair,
-                 inbound, landed, full, acts_s, grad_s, pair_s, pair_r, sum_s, sum_r, line_s, swap_s, near_r,
+                 inbound, landed, full, store, acts_s, grad_s, pair_s, pair_r, sum_s, sum_r, line_s, swap_s, near_r,
                  side_s, side_r):
     chips = n // 2
     nhalf = nblocks // 2
@@ -192,15 +294,15 @@
         down_first = jnp.where(p < nown, 2 * p, 2 * (p - nown) + 1)
         return jnp.where(first, up_first, jnp.where(last, down_first, natural))
 
+    greet_wait = greet(
+        [(None, {"dp": pair}), (chip > 0, {"dp": low}), (chip < chips - 1, {"dp": high})]
+        + [(None, {"pipe": lax.rem(section + step, sections)}) for step in range(1, sections)]
+    )
+
     for p in range(nhalf):
         acts_copy(turn_of(p)).start()
     grad_copy = pltpu.make_async_copy(grad, grad_v, grad_s)
     grad_copy.start()
-
-    greet(
-        [(None, {"dp": pair}), (chip > 0, {"dp": low}), (chip < chips - 1, {"dp": high})]
-        + [(None, {"pipe": lax.rem(section + step, sections)}) for step in range(1, sections)]
-    )
 
     def partial(block, ref):
         x = acts_v[:, pl.ds(pl.multiple_of(block * BLK, BLK), BLK)]
@@ -218,7 +320,7 @@
         mine[t] = mine[t] + from_pair[t]
 
     def piece(k):
-        return pl.ds(k * CHUNK, CHUNK)
+        return pl.ds(*PIECES[k])
 
     def sum_copy(t, k, target):
         return pltpu.make_async_remote_copy(
@@ -234,21 +336,30 @@
 
         sum_copy(t, k, target).start()
 
+    def take_turn(p):
+        t = turn_of(p)
+        acts_copy(t).wait()
+        partial(2 * t + 1 - core, theirs.at[t])
+        pair_copy(t).start()
+        partial(2 * t + core, mine.at[t])
+
+    start_t = turn_of(0)
+    acts_copy(start_t).wait()
+    partial(2 * start_t + 1 - core, theirs.at[start_t])
+    partial(2 * start_t + core, mine.at[start_t])
+    greet_wait()
+    pair_copy(start_t).start()
+
     @pl.loop(0, nown + chips)
     def _(tick):
-        for p in (2 * tick, 2 * tick + 1):
-            @pl.when(p < nhalf)
-            def _():
-                t = turn_of(p)
-                acts_copy(t).wait()
-                partial(2 * t + 1 - core, theirs.at[t])
-                pair_copy(t).start()
-                partial(2 * t + core, mine.at[t])
-
-        i = tick - 1 - chip
+        @pl.when(2 * tick + 1 < nhalf)
+        def _():
+            take_turn(2 * tick + 1)
+
+        i = tick - chip
         t = 2 * i + 1
         rising = (i >= 0) & (t < nhalf) & jnp.logical_not(last)
-        j = tick - 1 - (chips - 1 - chip)
+        j = tick - (chips - 1 - chip)
         u = 2 * j
         falling = (j >= 0) & (u < nhalf) & jnp.logical_not(first)
 
@@ -268,6 +379,10 @@
             @pl.when(falling)
             def _():
                 pass_sum(u, k, last, low)
+
+        @pl.when(2 * tick + 2 < nhalf)
+        def _():
+            take_turn(2 * tick + 2)
 
     def close_sum(t):
         fold_pair(t)
@@ -277,7 +392,7 @@
 
     def invert(slots):
         own = [2 * slot + is_last for slot in slots]
-        b11, b21, b22 = invert_parts([close_sum(t) for t in own], tokens)
+        b11, b21, b22 = invert_parts([close_sum(t) for t in own], tokens, store)
         for i, t in enumerate(own):
             pack_into(landed.at[2 * t + core], b11[i], b21[i], b22[i])
 
@@ -379,12 +494,12 @@
                 def _():
                     grad_copy.wait()
 
-            if k == 1:
+            if k == CHUNKS // 2:
                 @pl.when(rose)
                 def _():
                     both_products(t - 2)
 
-            if k == 2:
+            if k == CHUNKS - 1:
                 @pl.when(rising)
                 def _():
                     open_block(2 * t + core)
@@ -425,10 +540,12 @@
             ).wait_recv()
 
 
-def emit_kernel(owners, values, rows, precond, held, slots, zeros, copy_s, held_s):
+def emit_kernel(owner_of, values, rows, precond, held, owners, slots, zeros, copy_s, held_s, owner_s):
     section = lax.axis_index("pipe")
-    sections, nblocks = owners.shape
+    sections, nblocks = owner_of.shape
     total = sections * nblocks
+    owner_copy = pltpu.make_async_copy(owner_of, owners, owner_s)
+    owner_copy.start()
     zeros[...] = jnp.zeros_like(zeros)
 
     def precond_copy(b):
@@ -440,6 +557,7 @@
 
     for j in range(HOST):
         slots[j] = -1
+    owner_copy.wait()
 
     def place(k, used):
         hit = owners[k // nblocks, lax.rem(k, nblocks)] == section
@@ -482,7 +600,6 @@
     share = BLK // n
     vmem = pl.BlockSpec(memory_space=pltpu.VMEM)
     hbm = pl.BlockSpec(memory_space=pltpu.HBM)
-    smem = pl.BlockSpec(memory_space=pltpu.SMEM)
     dma = pltpu.SemaphoreType.DMA
 
     values, rows = pl.pallas_call(
@@ -502,6 +619,7 @@
             pltpu.VMEM((nhalf, PACK, HALF), F32),
             pltpu.VMEM((nblocks, PACK, HALF), F32),
             pltpu.VMEM((nblocks, BLK, BLK), F32),
+            pltpu.VMEM((2, HALF, HALF), F32),
             dma((nhalf,)), dma, dma((nhalf,)), dma((nhalf,)), dma((nhalf, CHUNKS)), dma((nhalf, CHUNKS)),
             dma((nhalf, CHUNKS)), dma((nhalf, CHUNKS)), dma((nblocks, CHUNKS)),
             dma((nblocks, sections - 1)), dma((sections, nblocks)),
@@ -512,16 +630,19 @@
 
     precond, held = pl.pallas_call(
         emit_kernel,
-        in_specs=[smem, vmem, vmem],
+        in_specs=[hbm, vmem, vmem],
         out_specs=(hbm, hbm),
         out_shape=(
             jax.ShapeDtypeStruct((feature_count, columns), F32),
             jax.ShapeDtypeStruct((HOST, share, BLK), F32),
         ),
-        scratch_shapes=[pltpu.SMEM((HOST,), jnp.int32), pltpu.VMEM((share, BLK), F32), dma((nblocks,)), dma((HOST,))],
+        scratch_shapes=[
+            pltpu.SMEM(owner_of.shape, jnp.int32), pltpu.SMEM((HOST,), jnp.int32), pltpu.VMEM((share, BLK), F32),
+            dma((nblocks,)), dma((HOST,)), dma,
+        ],
         compiler_params=pltpu.CompilerParams(vmem_limit_bytes=16 * 2**20),
         name="emit_outputs",
-    )(owner_of, values, rows)
+    )(pltpu.with_memory_space_constraint(owner_of, pltpu.HBM), values, rows)
     return precond, held[None]
 
 

time: 65.3 us -> 60.5 us (0.926)
  Pallas kernels: 64.5 us -> 59.7 us
    pallas_call x1, Pallas kernels: 60.7 us -> 56.5 us  [shards(): pl.pallas_call(functools.partial(solve_kernel, n, sections, nblocks, floa...]
where the time goes in v3:
time: 60.5 us; the launch traced here: 60.4 us
  Pallas kernels  59.7 us (99%)
  between operations  0.64 us (1%)
    pallas_call x1, Pallas kernels, shards(): pl.pallas_call(functools.partial(solve_kernel, n, sections, nblocks, floa...  56.5 us
    pallas_call x1, Pallas kernels, shards(): pl.pallas_call(emit_kernel, in_specs=[hbm, vmem, vmem], out_specs=(hbm, h...  3.19 us

profile of v3, /device:TPU:0, one launch (start us, length us, event | category | flops | bytes accessed | tf_op | source)
XLA Modules:
  0.0 60.4 jit_solution(724973643105948197)
XLA Ops:
  0.6 56.5 %solve_blocks.1 = (f32[3072,512]{1,0:T(8,128)S(1)}, f32[4,12,32,256]{3,2,1,0:T(8,128)S(1)}) custom-call(bf16[256,3072]{1,0:T(8,128)(2,1)} %bitcast.2, f32[3072,512]{1,0:T(8,128)} %grad.1), custom_call_target="tpu_custom_call" | custom-call | tf_op jit(solution)/shard_map/solve_blocks/pallas_call | solution.py:605
  57.2 3.2 %emit_outputs.1 = (f32[3072,512]{1,0:T(8,128)}, f32[24,32,256]{2,1,0:T(8,128)}) custom-call(s32[4,12]{1,0:T(4,128)} %owner_of.1, f32[3072,512]{1,0:T(8,128)S(1)} %get-tuple-element.6.values, f32[4,12,32,256]{3,2,1,0:T(8,128)S(1)} %get-tuple-element.7.rows), custom_call_target="tpu_custom_call" | custom-call | tf_op jit(solution)/shard_map/emit_outputs/pallas_call | solution.py:631
